TPU v7x, 32 devices: a whole 2x2x4 slice. The times are simulated.
32 devices in a mesh: pool: 2 (over core), dev: 16 (over z, y, x).
Axes of the slice: x: 2, y: 2, z: 4, core: 2. Of those that a mesh axis runs over, the one named last changes fastest.
Arguments:
- hidden: bfloat16 [256, 7168], P('dev'), may hold values from -240 to 240
- ffn_gain: float32 [7168], replicated, may hold values from 0.25 to 1.75
- final_gain: float32 [7168], replicated, may hold values from 0.25 to 1.75
- pool_weights: bfloat16 [2, 16, 6144, 7168], P('pool', 'dev'), may hold values from -0.28347335 to 0.28347335
- expert_ids: int32 [256, 4], P('dev'), may hold values from 0 to 15, all different within a row; in each aligned block of 16 rows (0 to 15, 16 to 31, ...) at most 8 rows name the same one
- gate_weights: float32 [256, 4], P('dev'), may hold values from 0.05 to 0.6
- draft_ids: int32 [256], replicated, may hold values from 0 to 98303
Outputs:
- draft_logprob: float32 [256], replicated
Inputs may be any that keep to these rules, and one draw needn't show every extreme that they name: `expert_ids`: each row names 4 different experts. Within one owner's rows (aligned blocks of 16 rows) no expert is named by more than 8 rows; in some owners' rows an expert is named by exactly 8.
All inputs are finite; a program needn't handle non-finite values.
Results may differ from a plain program's by a relative error of at most 0.0008.
Values may be sent and summed in bfloat16 or wider, within the bound.
A program may use at most 192 MiB of HBM per device.

v0:
```python
import jax
import jax.numpy as jnp
from jax import lax
from jax.sharding import PartitionSpec as P

EXPERTS = 16


norm_eps = 1e-06
neg_fill = -1e30


def passed_along(shard, axis, by):
    length = lax.axis_size(axis)
    pairs = [(i, i + by) for i in range(length) if 0 <= i + by < length]
    return lax.ppermute(shard, axis, pairs)


def rms_norm(values_in, scale_gain):
    mean_square = jnp.mean(values_in * values_in, axis=-1, keepdims=True)
    return values_in * lax.rsqrt(mean_square + norm_eps) * scale_gain


def slot_index(expert_ids, capacity):
    tok_own, top_count = expert_ids.shape
    flat_ids = expert_ids.reshape(tok_own * top_count)
    onehot = (flat_ids[:, None] == jnp.arange(EXPERTS, dtype=jnp.int32)[None, :]).astype(jnp.int32)
    slot_rank = jnp.sum((jnp.cumsum(onehot, axis=0) - onehot) * onehot, axis=1)
    return flat_ids * capacity + slot_rank


def expert_block(in_rows, weights, active):
    ff_dev = weights.shape[0] // 3

    def compute(row_block):
        flat_rows = row_block.reshape(-1, row_block.shape[-1])
        gate_up = lax.dot_general(
            flat_rows,
            weights[: 2 * ff_dev],
            (((1,), (1,)), ((), ())),
            preferred_element_type=jnp.float32,
        )
        activated = (jax.nn.silu(gate_up[:, :ff_dev]) * gate_up[:, ff_dev:]).astype(jnp.bfloat16)
        projected = jnp.dot(activated, weights[2 * ff_dev :], preferred_element_type=jnp.float32)
        return projected.astype(jnp.bfloat16).reshape(row_block.shape)

    def skipped(row_block):
        return jnp.zeros_like(row_block)

    return lax.cond(active, compute, skipped, in_rows)


def shards(hidden, ffn_gain, final_gain, pool_weights, expert_ids, gate_weights, draft_ids):
    pool_id = lax.axis_index("pool")
    dev_id = lax.axis_index("dev")
    dev_count = lax.axis_size("dev")
    group_size = dev_count // EXPERTS
    tok_own = hidden.shape[0]
    capacity = tok_own // 2
    model_width = hidden.shape[1]
    weights = pool_weights[0, 0]
    rows_dev = weights.shape[0]
    expert_side = pool_id == 0
    attention_side = pool_id == 1
    residual = hidden.astype(jnp.float32)
    normed = rms_norm(residual, ffn_gain).astype(jnp.bfloat16)
    flat_slot = slot_index(expert_ids, capacity)
    slot_hits = flat_slot[:, None] == jnp.arange(EXPERTS * capacity, dtype=jnp.int32)[None, :]
    placing = jnp.any(slot_hits.reshape(tok_own, -1, EXPERTS * capacity), axis=1).astype(
        jnp.bfloat16
    )
    packed = lax.dot_general(
        placing, normed, (((0,), (0,)), ((), ())), preferred_element_type=jnp.float32
    ).astype(jnp.bfloat16)
    copies = jnp.broadcast_to(
        packed.reshape(EXPERTS, 1, capacity, model_width),
        (EXPERTS, group_size, capacity, model_width),
    )
    copies = copies.reshape(dev_count, capacity, model_width)
    partial_value = expert_block(
        lax.all_to_all(copies, "dev", split_axis=0, concat_axis=0, tiled=True), weights, expert_side
    )
    returned = lax.all_to_all(partial_value, "dev", split_axis=0, concat_axis=0, tiled=True)
    summed = jnp.sum(
        returned.reshape(EXPERTS, group_size, capacity, model_width), axis=1, dtype=jnp.float32
    )
    summed = summed.reshape(EXPERTS * capacity, model_width)
    arrived_rows = passed_along(summed, "pool", 1)
    picked = jnp.take(arrived_rows, flat_slot, axis=0).reshape(tok_own, -1, model_width)
    mixture = jnp.sum(picked * gate_weights[:, :, None], axis=1)
    final_rows = rms_norm(residual + mixture, final_gain).astype(jnp.bfloat16)
    local_target = draft_ids - dev_id * rows_dev
    columns = jnp.arange(rows_dev, dtype=jnp.int32)

    def shard_logits(row_piece):
        return lax.dot_general(
            row_piece, weights, (((1,), (1,)), ((), ())), preferred_element_type=jnp.float32
        )

    def filler(row_block):
        return jnp.full((row_block.shape[0], rows_dev), neg_fill, jnp.float32)

    new_part = lax.cond(
        attention_side, shard_logits, filler, lax.all_gather(final_rows, "dev", axis=0, tiled=True)
    )
    row_max = lax.pmax(jnp.max(new_part, axis=1), ("pool", "dev"))
    shifted = jnp.sum(jnp.exp(new_part - row_max[:, None]), axis=1)
    picked_logit = jnp.sum(
        jnp.where(columns[None, :] == local_target[:, None], new_part, 0.0), axis=1
    )
    picked_logit = jnp.where(attention_side, picked_logit, 0.0)
    exp_total, target = lax.psum((shifted, picked_logit), ("pool", "dev"))
    return target - row_max - jnp.log(exp_total)


def solution(mesh):
    return jax.shard_map(
        shards,
        mesh=mesh,
        in_specs=(
            P("dev", None),
            P(),
            P(),
            P("pool", "dev", None, None),
            P("dev", None),
            P("dev", None),
            P(),
        ),
        out_specs=P(),
        check_vma=False,
    )
```

profile of v0, /device:TPU:0, one launch (start us, length us, event | category | flops | bytes accessed | tf_op | source)
XLA Modules:
  0.0 347.9 jit_solution(18419007125955180463)
XLA Ops:
  6.5 0.8 copy.14
  7.3 0.1 reshape.98
  7.4 0.1 fusion.22
  7.5 0.1 reduce_window_sum.11
  7.6 0.2 select_reduce_fusion.1
  7.7 0.1 reduce_sum.63
  7.9 0.1 copy.16
  7.9 0.1 fusion.23
  8.0 1.1 fusion.16
  9.1 2.9 fusion.15
  12.0 8.3 %all-to-all-start = ((bf16[16,8,7168]{2,1,0:T(8,128)(2,1)}), bf16[16,8,7168]{2,1,0:T(8,128)(2,1)S(1)}, u32[]{:S(2)}, u32[]{:S(2)}) async-start(bf16[16,8,7168]{2,1,0:T(8,128)(2,1)} %fusion.15), calls=%async_computation | async-start | bytes 3670016 | tf_op jit(solution)/shard_map/all_to_all | solution.py:81
  20.4 0.0 all-gather.2.cloned.1.call-start
  20.4 38.5 %all-to-all-done = bf16[16,8,7168]{2,1,0:T(8,128)(2,1)S(1)} async-done(((bf16[16,8,7168]{2,1,0:T(8,128)(2,1)}), bf16[16,8,7168]{2,1,0:T(8,128)(2,1)S(1)}, u32[]{:S(2)}, u32[]{:S(2)}) %all-to-all-start) | async-done | bytes 1835040 | tf_op jit(solution)/shard_map/all_to_all | solution.py:81
  58.9 38.5 %conditional.2 = (bf16[16,8,7168]{2,1,0:T(8,128)(2,1)S(1)}) conditional(s32[]{:T(128)} %convert_element_type.33, () %tuple.18, (bf16[16,8,7168]{2,1,0:T(8,128)(2,1)S(1)}, bf16[6144,7168]{1,0:T(8,128)(2,1)}) %tuple.19), branch_computations={%region_4.5_spmd, %region_5.6_spmd} | conditional | flops 11276779520 | bytes 95944712 | solution.py:50
  58.9 26.3 %fusion = f32[128,4096]{1,0:T(8,128)} fusion(bf16[6144,7168]{1,0:T(8,128)(2,1)} %get-tuple-element.20, bf16[16,8,7168]{2,1,0:T(8,128)(2,1)S(1)} %get-tuple-element.18), kind=kOutput, calls=%fused_computation.1 | convolution fusion | flops 7516192768 | bytes 62652416 | tf_op jit(solution)/shard_map/cond/branch_1_fun/dot_general | solution.py:37
  85.2 12.2 %fusion.7 = bf16[16,8,7168]{2,1,0:T(8,128)(2,1)S(1)} fusion(bf16[6144,7168]{1,0:T(8,128)(2,1)} %get-tuple-element.20, f32[128,4096]{1,0:T(8,128)} %fusion), kind=kOutput, calls=%fused_computation.6 | convolution fusion | flops 3760586752 | bytes 33292288 | tf_op jit(solution)/shard_map/cond/branch_1_fun/dot_general | solution.py:44
  97.4 34.3 %all_to_all.10 = bf16[16,8,7168]{2,1,0:T(8,128)(2,1)S(1)} all-to-all(bf16[16,8,7168]{2,1,0:T(8,128)(2,1)S(1)} %get-tuple-element.29), channel_id=1, replica_groups=mesh['pool'=2,'dev'=16] {'dev'}, dimensions={0} | all-to-all | bytes 3670016 | tf_op jit(solution)/shard_map/all_to_all | solution.py:83
  131.7 0.0 copy-start.2
  131.7 2.2 bitcast_convert_fusion
  133.9 3.1 collective-permute-start
  137.0 0.1 mul.90
  137.1 0.0 copy-done.2
  137.1 0.1 copy.17
  137.2 4.3 %collective-permute-done = f32[128,7168]{1,0:T(8,128)} collective-permute-done((f32[128,7168]{1,0:T(8,128)}, f32[128,7168]{1,0:T(8,128)}, u32[]{:S(2)}, u32[]{:S(2)}) %collective-permute-start) | collective-permute-done | bytes 3670048 | tf_op jit(solution)/shard_map/ppermute | solution.py:16
  141.5 4.0 %gather_fusion = f32[64,7168]{1,0:T(8,128)S(1)} fusion(f32[128,7168]{1,0:T(8,128)} %collective-permute-done, s32[1024]{0:T(1024)S(1)} %pad_clamp_fusion), kind=kCustom, calls=%fused_computation | custom fusion | bytes 3670272 | tf_op jit(solution)/shard_map/jit(_take)/gather | solution.py:89
  145.6 0.0 copy-start
  145.6 0.0 copy-start.1
  145.6 0.0 copy-start.3
  145.6 1.8 gather.7
  147.4 2.9 multiply_reduce_fusion
  150.3 0.0 copy-done
  150.3 0.2 multiply_reduce_fusion.1
  150.5 0.0 copy-done.1
  150.5 0.8 multiply_convert_fusion
  151.3 0.0 all-gather.2.cloned.1.call-update
  151.3 0.0 copy-done.3
  151.4 69.6 %all-gather.2.cloned.1.call-done = bf16[256,7168]{1,0:T(8,128)(2,1)} async-done(((bf16[16,7168]{1,0:T(8,128)(2,1)}), bf16[256,7168]{1,0:T(8,128)(2,1)}) %all-gather.2.cloned.1.call-update) | async-done | bytes 3670032 | tf_op jit(solution)/shard_map/all_gather | solution.py:104
  220.9 3.4 conditional.3
  220.9 3.4 broadcast.91
  224.3 3.2 reduce_max.9
  227.5 70.0 %pmax.7 = f32[256]{0:T(256)S(1)} all-reduce(f32[256]{0:T(256)S(1)} %reduce_max.9), channel_id=1, replica_groups=mesh['pool'=2,'dev'=16] {'pool','dev'}, use_global_device_ids=true, to_apply=%region_13.14 | all-reduce | flops 256 | bytes 2048 | tf_op jit(solution)/shard_map/pmax | solution.py:106
  297.5 3.8 %select_reduce_fusion = (f32[256]{0:T(256)S(1)}, f32[256]{0:T(256)S(1)}) fusion(f32[256,6144]{1,0:T(8,128)} %get-tuple-element.30, s32[256]{0:T(256)S(1)} %broadcast_subtract_fusion, f32[256]{0:T(256)S(1)} %pmax.7), kind=kLoop, calls=%fused_computation.15 | loop fusion | flops 7863808 | bytes 6295552 | tf_op jit(solution)/shard_map/reduce_sum | solution.py:108
  301.3 39.1 %all-reduce = (f32[256]{0:T(256)S(1)}, f32[256]{0:T(256)S(1)}) all-reduce(f32[256]{0:T(256)S(1)} %get-tuple-element.24, f32[256]{0:T(256)S(1)} %broadcast_select_fusion), channel_id=1, replica_groups=mesh['pool'=2,'dev'=16] {'pool','dev'}, use_global_device_ids=true, to_apply=%region_15.16 | all-reduce | flops 512 | bytes 4096 | tf_op jit(solution)/shard_map/psum | solution.py:112
  340.5 0.6 log_subtract_fusion
  (8 shorter events, 0.1 us)
Async XLA Ops:
  12.0 46.9 %all-to-all-start = ((bf16[16,8,7168]{2,1,0:T(8,128)(2,1)}), bf16[16,8,7168]{2,1,0:T(8,128)(2,1)S(1)}, u32[]{:S(2)}, u32[]{:S(2)}) async-start(bf16[16,8,7168]{2,1,0:T(8,128)(2,1)} %fusion.15), calls=%async_computation | async-start | bytes 3670016 | tf_op jit(solution)/shard_map/all_to_all | solution.py:81
  20.4 200.6 %all-gather.2.cloned.1.call-start = ((), (), s32[]{:S(2)}) async-start(), calls=%async_computation.2 | async-start | bytes 3899392 | tf_op jit(solution)/shard_map/all_gather | solution.py:104
  131.7 5.4 %copy-start.2 = (f32[16,4]{0,1:T(4,128)S(1)}, f32[16,4]{0,1:T(4,128)}, u32[]{:S(2)}) copy-start(f32[16,4]{0,1:T(4,128)} %param.16) | copy-start | bytes 772
  133.9 7.6 %collective-permute-start = (f32[128,7168]{1,0:T(8,128)}, f32[128,7168]{1,0:T(8,128)}, u32[]{:S(2)}, u32[]{:S(2)}) collective-permute-start(f32[128,7168]{1,0:T(8,128)} %bitcast_convert_fusion), channel_id=1, source_target_pairs={{0,16},{1,17},{2,18},{3,19},{4,20},{5,21},{6,22},{7,23},{8,24},{9,... | collective-permute-start | bytes 11010056 | tf_op jit(solution)/shard_map/ppermute | solution.py:16
  145.6 4.7 %copy-start = (bf16[16,7168]{1,0:T(8,128)(2,1)S(1)}, bf16[16,7168]{1,0:T(8,128)(2,1)}, u32[]{:S(2)}) copy-start(bf16[16,7168]{1,0:T(8,128)(2,1)} %param.11) | copy-start | bytes 688132
  145.6 4.9 %copy-start.1 = (f32[7168]{0:T(1024)S(1)}, f32[7168]{0:T(1024)}, u32[]{:S(2)}) copy-start(f32[7168]{0:T(1024)} %param.13) | copy-start | bytes 86020
  145.6 5.8 %copy-start.3 = (s32[256]{0:T(256)S(1)}, s32[256]{0:T(256)}, u32[]{:S(2)}) copy-start(s32[256]{0:T(256)} %param.17) | copy-start | bytes 3076
Sparse Core Ops, SparseCore 0:
  151.5 69.4 all-gather.1
where the time goes:
time: 348 us
  blocking collectives  143 us (41%)
  waiting for transfers between devices  112 us (32%)
  matrix products  41.4 us (12%)
  other arithmetic  15.2 us (4%)
  between operations  13.5 us (4%)
  starting transfers between devices  11.5 us (3%)
  local copies, waits for them, and re-layouts  10.4 us (3%)
    pmax x1, blocking collectives, shards(): row_max = lax.pmax(jnp.max(new_part, axis=1), ('pool', 'dev'))  70 us
    all_gather x1, waiting for transfers between devices, shards(): lax.all_gather(final_rows, 'dev', axis=0, tiled=True)  69.6 us
    psum x1, blocking collectives, shards(): exp_total, target = lax.psum((shifted, picked_logit), ('pool', 'dev'))  39.1 us
    all_to_all x1, waiting for transfers between devices, shards(): lax.all_to_all(copies, 'dev', split_axis=0, concat_axis=0, tiled=True)  38.5 us
    all_to_all x1, blocking collectives, shards(): lax.all_to_all(partial_value, 'dev', split_axis=0, concat_axis=0, tiled=T...  34.3 us
    dot_general x1, matrix products, compute(): lax.dot_general(flat_rows, weights[:2 * ff_dev], (((1,), (1,)), ((), ()))...  26.3 us
    dot_general x1, matrix products, compute(): jnp.dot(activated, weights[2 * ff_dev:], preferred_element_type=jnp.float32)  12.2 us
    all_to_all x1, starting transfers between devices, shards(): lax.all_to_all(copies, 'dev', split_axis=0, concat_axis=0, tiled=True)  8.34 us
  transfers between devices with their start and end apart: 3, of which 3 were waited for; matrix products, arithmetic and copies ran while one was open for 0% of the time, Pallas kernels for 0%

commit v1 on v0

v1 whole, which is shorter than its diff:
```python
import functools

import jax
import jax.numpy as jnp
from jax import lax
from jax.experimental import pallas as pl
from jax.experimental.pallas import tpu as pltpu
from jax.sharding import PartitionSpec as P

EXPERTS = 16
LANES = 128
COLS = 512
LINE = 4
MESH = pl.DeviceIdType.MESH

norm_eps = 1e-06
neg_fill = -1e30


def rms_norm(values_in, scale_gain):
    mean_square = jnp.mean(values_in * values_in, axis=-1, keepdims=True)
    return values_in * lax.rsqrt(mean_square + norm_eps) * scale_gain


def kernel(
    n, slots, hidden_ref, ffn_gain_ref, final_gain_ref, placing_ref, mixing_ref, draft_ref, w_hbm,
    out_ref,
    w_buf, packed, landed, part, x_buf, act, final_buf, stat_out, stat_all, result,
    tops, sums, picks,
    w_sem, s1_send, s1_recv, s2_send, s2_recv, ag_send, ag_recv, st_send, st_recv, res_send, res_recv,
):
    pool = lax.axis_index("pool")
    me = lax.axis_index("dev")
    group = n // EXPERTS
    tile = w_buf.shape[1]
    rows_dev, width = w_hbm.shape
    tiles = rows_dev // tile
    ff_tiles = tiles // 3
    capacity = packed.shape[1]
    tok_own = hidden_ref.shape[0]
    flat = n * capacity

    def fetch(row_tile, slot):
        start = pl.multiple_of(row_tile * tile, tile)
        return pltpu.make_async_copy(w_hbm.at[pl.ds(start, tile)], w_buf.at[slot], w_sem.at[slot])

    def send(src, dst, send_sem, recv_sem, to_pool, to_dev):
        return pltpu.make_async_remote_copy(
            src_ref=src, dst_ref=dst, send_sem=send_sem, recv_sem=recv_sem,
            device_id=(to_pool, to_dev), device_id_type=MESH,
        )

    def expert_order(t):
        return jnp.where(t < 2 * ff_tiles, (t % 2) * ff_tiles + t // 2, t)

    @pl.when(pool == 0)
    def _():
        normed = rms_norm(hidden_ref[...].astype(jnp.float32), ffn_gain_ref[...]).astype(jnp.bfloat16)
        rows = jnp.dot(placing_ref[...], normed, preferred_element_type=jnp.float32)
        packed[...] = rows.reshape(packed.shape).astype(jnp.bfloat16)
        out_copies = []
        for k in range(1, n):
            to = lax.rem(me + k, n)
            c = send(packed.at[to // group], landed.at[me], s1_send.at[k], s1_recv.at[me], 0, to)
            c.start()
            out_copies.append(c)
        for t in range(slots):
            fetch(expert_order(jnp.int32(t)), t).start()
        landed[me] = packed[me // group]
        for k in range(1, n):
            src = lax.rem(me + n - k, n)
            send(packed.at[0], landed.at[src], s1_send.at[k], s1_recv.at[src], 0, src).wait_recv()
        for c in out_copies:
            c.wait_send()

        def unpack(c, _):
            cols = pl.ds(pl.multiple_of(c * COLS, COLS), COLS)
            x_buf[:flat, cols] = (
                landed[:, :, cols].astype(jnp.float32).reshape(flat, COLS).astype(jnp.bfloat16)
            )
            return 0

        lax.fori_loop(0, width // COLS, unpack, 0)

        def gate_up(j, _):
            halves = []
            for h in range(2):
                t = 2 * j + h
                slot = lax.rem(t, slots)
                fetch(0, slot).wait()
                halves.append(
                    lax.dot_general(
                        x_buf[:flat], w_buf[slot], (((1,), (1,)), ((), ())),
                        preferred_element_type=jnp.float32,
                    )
                )

                @pl.when(t + slots < tiles)
                def _():
                    fetch(expert_order(t + slots), slot).start()

            gate, up = halves
            act[j] = (gate / (1.0 + jnp.exp(-gate)) * up).astype(jnp.bfloat16)
            return 0

        lax.fori_loop(0, ff_tiles, gate_up, 0)
        for t in range(2 * ff_tiles, tiles):
            fetch(0, t % slots).wait()

        def down(c, _):
            cols = pl.ds(pl.multiple_of(c * COLS, COLS), COLS)
            total = jnp.zeros((flat, COLS), jnp.float32)
            for i in range(ff_tiles):
                total += jnp.dot(
                    act[i], w_buf[(2 * ff_tiles + i) % slots, :, cols],
                    preferred_element_type=jnp.float32,
                )
            part[:, :, cols] = total.reshape(n, capacity, COLS).astype(jnp.bfloat16)
            return 0

        lax.fori_loop(0, width // COLS, down, 0)
        back = []
        for k in range(n):
            to = lax.rem(me + k, n)
            c = send(part.at[to], landed.at[me], s2_send.at[k], s2_recv.at[me], 1, to)
            c.start()
            back.append(c)
        for c in back:
            c.wait_send()
        send(result, result, res_send, res_recv, 1, me).wait_recv()

    @pl.when(pool == 1)
    def _():
        for t in range(slots):
            fetch(t, t).start()
        for k in range(n):
            src = lax.rem(me + n - k, n)
            send(part.at[0], landed.at[src], s2_send.at[k], s2_recv.at[src], 0, src).wait_recv()
        mix = mixing_ref[...]
        high = mix.astype(jnp.bfloat16)
        rest = mix - high.astype(jnp.float32)
        mid = rest.astype(jnp.bfloat16)
        low = (rest - mid.astype(jnp.float32)).astype(jnp.bfloat16)

        def combine(c, square):
            cols = pl.ds(pl.multiple_of(c * COLS, COLS), COLS)
            rows = landed[:, :, cols].astype(jnp.float32).reshape(flat, COLS).astype(jnp.bfloat16)
            moe = jnp.dot(high, rows, preferred_element_type=jnp.float32)
            moe += jnp.dot(mid, rows, preferred_element_type=jnp.float32)
            moe += jnp.dot(low, rows, preferred_element_type=jnp.float32)
            final = hidden_ref[:, cols].astype(jnp.float32) + moe
            final_buf[:, cols] = final
            return square + jnp.sum(final * final, axis=1, keepdims=True)

        square = lax.fori_loop(0, width // COLS, combine, jnp.zeros((tok_own, 1), jnp.float32))
        scale = lax.rsqrt(square / width + norm_eps)
        mine = pl.ds(pl.multiple_of(me * tok_own, tok_own), tok_own)
        x_buf[mine] = (final_buf[...] * scale * final_gain_ref[...]).astype(jnp.bfloat16)

        lines = n // LINE
        hi, lo = me // LINE, lax.rem(me, LINE)

        def rows_of(dev):
            return pl.ds(pl.multiple_of(dev * tok_own, tok_own), tok_own)

        sent = []
        count = 0

        def push(owner, to):
            nonlocal count
            c = send(
                x_buf.at[rows_of(owner)], x_buf.at[rows_of(owner)],
                ag_send.at[count], ag_recv.at[owner], 1, to,
            )
            c.start()
            count += 1
            sent.append(c)

        def arrive(owner):
            send(
                x_buf.at[rows_of(owner)], x_buf.at[rows_of(owner)],
                ag_send.at[0], ag_recv.at[owner], 1, owner,
            ).wait_recv()

        for h in range(1, lines):
            push(me, lax.rem(hi + h, lines) * LINE + lo)
        for h in range(lines):
            owner = lax.rem(hi + lines - h, lines) * LINE + lo
            if h:
                arrive(owner)
            for l in range(1, LINE):
                push(owner, hi * LINE + lax.rem(lo + l, LINE))
        for h in range(lines):
            for l in range(1, LINE):
                arrive(lax.rem(hi + lines - h, lines) * LINE + lax.rem(lo + LINE - l, LINE))
        for c in sent:
            c.wait_send()

        tops[...] = jnp.full_like(tops, neg_fill)
        sums[...] = jnp.zeros_like(sums)
        picks[...] = jnp.zeros_like(picks)

        def score(t, _):
            slot = lax.rem(t, slots)
            fetch(0, slot).wait()
            logits = lax.dot_general(
                x_buf[...], w_buf[slot], (((1,), (1,)), ((), ())),
                preferred_element_type=jnp.float32,
            )

            @pl.when(t + slots < tiles)
            def _():
                fetch(t + slots, slot).start()

            target = draft_ref[...] - (me * rows_dev + t * tile)
            lane = lax.broadcasted_iota(jnp.int32, (logits.shape[0], LANES), 1)
            pieces = [logits[:, i * LANES : (i + 1) * LANES] for i in range(tile // LANES)]
            old = tops[...]
            top = functools.reduce(jnp.maximum, pieces, old)
            total = sums[...] * jnp.exp(old - top)
            pick = picks[...]
            for i, piece in enumerate(pieces):
                total += jnp.exp(piece - top)
                pick += jnp.where(lane + i * LANES == target, piece, 0.0)
            tops[...] = top
            sums[...] = total
            picks[...] = pick
            return 0

        lax.fori_loop(0, tiles, score, 0)
        tall = tops[...].T
        top = jnp.max(tall, axis=0, keepdims=True)
        total = jnp.sum(sums[...].T * jnp.exp(tall - top), axis=0, keepdims=True)
        pick = jnp.sum(picks[...].T, axis=0, keepdims=True)
        mine_stats = jnp.concatenate([top, total, pick, jnp.zeros((5, top.shape[1]), jnp.float32)], axis=0)
        stat_out[...] = mine_stats
        told = []
        for k in range(1, n):
            to = lax.rem(me + k, n)
            c = send(stat_out, stat_all.at[me], st_send.at[k], st_recv.at[me], 1, to)
            c.start()
            told.append(c)
        stat_all[me] = mine_stats
        for k in range(1, n):
            src = lax.rem(me + n - k, n)
            send(stat_out, stat_all.at[src], st_send.at[k], st_recv.at[src], 1, src).wait_recv()
        every = stat_all[...]
        best = jnp.max(every[:, 0:1, :], axis=0)
        exp_total = jnp.sum(every[:, 1:2, :] * jnp.exp(every[:, 0:1, :] - best[None]), axis=0)
        drafted = jnp.sum(every[:, 2:3, :], axis=0)
        result[...] = jnp.broadcast_to(drafted - best - jnp.log(exp_total), result.shape)
        c = send(result, result, res_send, res_recv, 0, me)
        c.start()
        for d in told:
            d.wait_send()
        c.wait_send()

    out_ref[...] = result[...]


def shards(hidden, ffn_gain, final_gain, pool_weights, expert_ids, gate_weights, draft_ids):
    n = lax.axis_size("dev")
    group = n // EXPERTS
    tok_own, width = hidden.shape
    capacity = tok_own // 2
    tokens = draft_ids.shape[0]
    weights = pool_weights[0, 0]
    rows_dev = weights.shape[0]
    tile = 512 if n <= 16 else 256
    slots = min(6 if n <= 16 else 4, rows_dev // tile)
    top_count = expert_ids.shape[1]
    places = EXPERTS * capacity

    onehot = (expert_ids[:, :, None] == jnp.arange(EXPERTS, dtype=jnp.int32)).astype(jnp.int32)
    named = jnp.sum(onehot, axis=1)
    earlier = jnp.arange(tok_own)[:, None] > jnp.arange(tok_own)[None, :]
    before = jnp.sum(jnp.where(earlier[:, :, None], named[None], 0), axis=1)
    rank = jnp.sum(onehot * before[:, None, :], axis=2)
    flat_slot = expert_ids * capacity + rank
    hits = flat_slot[:, :, None] == jnp.arange(places, dtype=jnp.int32)
    placing = jnp.any(hits, axis=1).astype(jnp.bfloat16).T
    mixing = jnp.sum(jnp.where(hits, gate_weights[:, :, None], 0.0), axis=1)
    mixing = jnp.broadcast_to(
        mixing.reshape(tok_own, EXPERTS, 1, capacity), (tok_own, EXPERTS, group, capacity)
    ).reshape(tok_own, n * capacity)

    vmem = pl.BlockSpec(memory_space=pltpu.VMEM)
    dma = pltpu.SemaphoreType.DMA
    lines = n // LINE
    out = pl.pallas_call(
        functools.partial(kernel, n, slots),
        out_shape=jax.ShapeDtypeStruct((8, tokens), jnp.float32),
        in_specs=[vmem] * 6 + [pl.BlockSpec(memory_space=pl.ANY)],
        out_specs=vmem,
        scratch_shapes=[
            pltpu.VMEM((slots, tile, width), jnp.bfloat16),
            pltpu.VMEM((EXPERTS, capacity, width), jnp.bfloat16),
            pltpu.VMEM((n, capacity, width), jnp.bfloat16),
            pltpu.VMEM((n, capacity, width), jnp.bfloat16),
            pltpu.VMEM((tokens, width), jnp.bfloat16),
            pltpu.VMEM((rows_dev // 3 // tile, n * capacity, tile), jnp.bfloat16),
            pltpu.VMEM((tok_own, width), jnp.float32),
            pltpu.VMEM((8, tokens), jnp.float32),
            pltpu.VMEM((n, 8, tokens), jnp.float32),
            pltpu.VMEM((8, tokens), jnp.float32),
            pltpu.VMEM((tokens, LANES), jnp.float32),
            pltpu.VMEM((tokens, LANES), jnp.float32),
            pltpu.VMEM((tokens, LANES), jnp.float32),
            dma((slots,)),
            dma((n,)), dma((n,)), dma((n,)), dma((n,)),
            dma((n + lines,)), dma((n,)),
            dma((n,)), dma((n,)), dma, dma,
        ],
        compiler_params=pltpu.CompilerParams(has_side_effects=True, vmem_limit_bytes=66_000_000),
    )(
        hidden, ffn_gain[None], final_gain[None], placing, mixing, draft_ids[:, None], weights,
    )
    return out[0]


def solution(mesh):
    return jax.shard_map(
        shards,
        mesh=mesh,
        in_specs=(
            P("dev", None),
            P(),
            P(),
            P("pool", "dev", None, None),
            P("dev", None),
            P("dev", None),
            P(),
        ),
        out_specs=P(),
        check_vma=False,
    )
```

time: 348 us -> 152 us (0.44)
  Pallas kernels: 0 us -> 144 us
  blocking collectives: 143 us -> 0 us
  waiting for transfers between devices: 112 us -> 0 us
  matrix products: 41.4 us -> 0 us
  between operations: 13.5 us -> 0.04 us
  starting transfers between devices: 11.5 us -> 0 us
  other arithmetic: 15.2 us -> 3.91 us
  local copies, waits for them, and re-layouts: 10.4 us -> 3.42 us
    pallas_call x0 -> x1, Pallas kernels: none -> 144 us  [shards(): pl.pallas_call(functools.partial(kernel, n, slots), out_shape=jax.ShapeDt...]
    pmax x1 -> x0, blocking collectives: 70 us -> none  [shards(): row_max = lax.pmax(jnp.max(new_part, axis=1), ('pool', 'dev'))]
    all_gather x1 -> x0, waiting for transfers between devices: 69.6 us -> none  [shards(): lax.all_gather(final_rows, 'dev', axis=0, tiled=True)]
    dot_general x3 -> x0, matrix products: 41.4 us -> none  [the longest x1 26.3 us: compute(): lax.dot_general(flat_rows, weights[:2 * ff_dev], (((1,), (1,)), ((), ()))...]
    psum x1 -> x0, blocking collectives: 39.1 us -> none  [shards(): exp_total, target = lax.psum((shifted, picked_logit), ('pool', 'dev'))]
    all_to_all x1 -> x0, waiting for transfers between devices: 38.5 us -> none  [shards(): lax.all_to_all(copies, 'dev', split_axis=0, concat_axis=0, tiled=True)]
    all_to_all x1 -> x0, blocking collectives: 34.3 us -> none  [shards(): lax.all_to_all(partial_value, 'dev', split_axis=0, concat_axis=0, tiled=T...]
    all_to_all x1 -> x0, starting transfers between devices: 8.34 us -> none  [shards(): lax.all_to_all(copies, 'dev', split_axis=0, concat_axis=0, tiled=True)]
  transfers between devices with their start and end apart: 3 -> 0, of which waited for: 3 -> 0; matrix products, arithmetic and copies ran while one was open for 0% -> 0% of each run, Pallas kernels for 0% -> 0%
where the time goes in v1:
time: 152 us
  Pallas kernels  144 us (95%)
  other arithmetic  3.91 us (3%)
  local copies, waits for them, and re-layouts  3.42 us (2%)
    pallas_call x1, Pallas kernels, shards(): pl.pallas_call(functools.partial(kernel, n, slots), out_shape=jax.ShapeDt...  144 us

profile of v1, /device:TPU:0, one launch (start us, length us, event | category | flops | bytes accessed | tf_op | source)
XLA Modules:
  0.0 151.8 jit_solution(12244285565815347862)
XLA Ops:
  0.0 0.8 convert_reduce_fusion
  0.8 0.1 select_reduce_fusion
  0.9 0.9 select_reduce_fusion.2
  1.8 0.7 multiply_add_fusion
  2.5 0.1 fusion
  2.6 1.4 select_reduce_fusion.1.mixing_ref
  3.9 0.7 copy.15
  4.6 1.5 copy.16.draft_ref
  6.1 144.4 %shard_map.73 = f32[8,256]{1,0:T(8,128)} custom-call(bf16[16,7168]{1,0:T(8,128)(2,1)} %hidden_ref.1, f32[1,7168]{1,0:T(1,128)} %bitcast.7, f32[1,7168]{1,0:T(1,128)} %bitcast.8, bf16[128,16]{1,0:T(8,128)(2,1)} %bitcast.6, f32[16,128]{1,0:T(8,128)} %select_reduce_fusion.1.mixing_ref, s32[256,1]{1,0:T(8,128)} %copy.16.draft_ref, bf16[6144,7168]{1,0:T(8,128)(2,1)} %bitcast.4.w_hbm), custom_call_target="tpu_custom_call" | custom-call | tf_op jit(solution)/shard_map/pallas_call | solution.py:290
  150.6 1.3 slice.3
  (2 shorter events, 0.0 us)
